TPU v7x, 32 devices: a whole 2x2x4 slice. The times are simulated.
32 devices in a mesh: dom: 8 (over y, x, core), shift: 4 (over z).
Axes of the slice: x: 2, y: 2, z: 4, core: 2. Of those that a mesh axis runs over, the one named last changes fastest.
Arguments:
- sources: float32 [32, 32, 16, 128], P('shift', 'dom'), may hold values from -6 to 6
- kappa: float32 [32, 16, 128], P('dom'), may hold values from 0 to 2
- mass: float32 [32, 16, 128], P('dom'), may hold values from 0.25 to 4
- shift_table: float32 [64], replicated, may hold values from 0.5 to 4
- shift_ids: int32 [16], P('shift'), may hold values from 0 to 63
- sketch: bfloat16 [1024, 32, 16, 128], P(None, 'dom'), may hold values from -0.1875 to 0.1875
Outputs:
- solution: float32 [16, 32, 32, 16, 128], P('shift', None, 'dom')
- residual: float32 [16, 32, 32, 16, 128], P('shift', None, 'dom')
Inputs may be any that keep to these rules, and one draw needn't show every extreme that they name: `shift_ids`: index into shift_table.
All inputs are finite; a program needn't handle non-finite values.
Results may differ from a plain program's by a relative error of at most 0.0026.
Values sent between devices are 32-bit elements; how exact they have to be, the bound alone decides.
A program may use at most 128 MiB of HBM per device.

v0:
```python
import functools

import jax
import jax.numpy as jnp
from jax import lax
from jax.experimental import pallas as pl
from jax.experimental.pallas import tpu as pltpu
from jax.sharding import PartitionSpec as P

HALO = 3
LANES = 128
MID = 2.25
BASIS = 10
IMAGES = ((1, 2), (3, 4, 5), (6, 7, 8, 9))
PAIRS = [(i, k) for i in range(BASIS) for k in range(i, BASIS)]
PAIR_INDEX = {pair: n for n, pair in enumerate(PAIRS)}


def neighbour_sum(field):
    inner = field[1:-1]
    shape = inner.shape
    total = field[2:] + field[:-2]
    for dim in (1, 2):
        size = shape[dim]
        place = lax.broadcasted_iota(jnp.int32, shape, dim)
        total = total + jnp.where(place > 0, pltpu.roll(inner, 1, dim), 0.0)
        total = total + jnp.where(place < size - 1, pltpu.roll(inner, size - 1, dim), 0.0)
    return total


def plane_mask(shape, width, low, high):
    plane = lax.broadcasted_iota(jnp.int32, shape, 0)
    return jnp.where(plane < width, low, jnp.where(plane >= shape[0] - width, high, 1.0))


def edge_flags():
    me = lax.axis_index("dom")
    last = lax.axis_size("dom") - 1
    return (me > 0).astype(jnp.float32), (me < last).astype(jnp.float32)


def basis_fields(w0, diag, mass, mask1, mask2):
    sixth = 1.0 / 6.0
    center = 6.0 + MID
    d1, m1 = diag[1:-1], mass[1:-1]
    d2, m2 = diag[2:-2], mass[2:-2]
    d3, m3 = diag[3:-3], mass[3:-3]
    w0i = w0[1:-1]
    a0 = d1 * w0i - neighbour_sum(w0)
    a1 = m1 * w0i
    scaled1 = sixth * mask1
    g0 = (a0 - center * w0i) * scaled1
    g1 = (a1 - w0i) * scaled1
    g0i, g1i = g0[1:-1], g1[1:-1]
    b0 = d2 * g0i - neighbour_sum(g0)
    b1 = d2 * g1i - neighbour_sum(g1) + m2 * g0i
    b2 = m2 * g1i
    scaled2 = sixth * mask2
    h0 = (b0 - center * g0i) * scaled2
    h1 = (b1 - center * g1i - g0i) * scaled2
    h2 = (b2 - g1i) * scaled2
    h0i, h1i, h2i = h0[1:-1], h1[1:-1], h2[1:-1]
    e0 = d3 * h0i - neighbour_sum(h0)
    e1 = d3 * h1i - neighbour_sum(h1) + m3 * h0i
    e2 = d3 * h2i - neighbour_sum(h2) + m3 * h1i
    e3 = m3 * h2i
    return [
        w0[3:-3], a0[2:-2], a1[2:-2], b0[1:-1], b1[1:-1], b2[1:-1], e0, e1, e2, e3
    ]


def solve_small(h_vals, entry):
    l00 = jnp.sqrt(entry[0][0])
    l10 = entry[1][0] / l00
    l20 = entry[2][0] / l00
    l11 = jnp.sqrt(entry[1][1] - l10 * l10)
    l21 = (entry[2][1] - l20 * l10) / l11
    l22 = jnp.sqrt(entry[2][2] - l20 * l20 - l21 * l21)
    f0 = h_vals[0] / l00
    f1 = (h_vals[1] - l10 * f0) / l11
    f2 = (h_vals[2] - l20 * f0 - l21 * f1) / l22
    c2 = f2 / l22
    c1 = (f1 - l21 * c2) / l11
    c0 = (f0 - l10 * c1 - l20 * c2) / l00
    return (c0, c1, c2)


def coefficients(gram, tau):
    def product(left, right):
        by_degree = {}
        for p, i in enumerate(left):
            for q, k in enumerate(right):
                n = PAIR_INDEX[(min(i, k), max(i, k))]
                column = gram[:, n : n + 1]
                by_degree[p + q] = by_degree[p + q] + column if p + q in by_degree else column
        top = max(by_degree)
        total = jnp.broadcast_to(by_degree[top], (gram.shape[0], LANES))
        for degree in range(top - 1, -1, -1):
            total = total * tau + by_degree[degree]
        return total

    h_vals = [product(image, (0,)) for image in IMAGES]
    entry = [[None] * 3 for _ in range(3)]
    for i in range(3):
        for k in range(i + 1):
            entry[i][k] = product(IMAGES[i], IMAGES[k])
    ridge = 0.001 * (entry[0][0] + entry[1][1] + entry[2][2]) / 3.0 + 1.0
    for i in range(3):
        entry[i][i] = entry[i][i] + ridge
    return solve_small(h_vals, entry)


def project_kernel(
    n, groups, src_ref, kappa_ref, mass_ref, table_ref, ids_ref, sketch_ref,
    wide_ref, coeff_ref, c_ref,
    rows_buf, raw_ref, fields_ref, out_buf, in_buf, gram_own, gram_in, gram_all,
    load_sem, z_send, z_recv, halo_send, halo_recv, km_send, km_recv,
    rs_send, rs_recv, g_send, g_recv, s_send, s_recv,
):
    me = lax.axis_index("dom")
    group = lax.axis_index("shift")
    nb, slab = src_ref.shape[0], src_ref.shape[1]
    block = rows_buf.shape[1]
    columns = BASIS * nb
    right, left = lax.rem(me + 1, n), lax.rem(me + n - 1, n)
    has_right, has_left = me < n - 1, me > 0

    def remote(src, dst, send, recv, **where):
        return pltpu.make_async_remote_copy(
            src_ref=src, dst_ref=dst, send_sem=send, recv_sem=recv,
            device_id=where, device_id_type=pl.DeviceIdType.MESH,
        )

    def load(t):
        owner = lax.rem(me + 1 + t, n)
        return pltpu.make_async_copy(
            sketch_ref.at[pl.ds(owner * block, block)], rows_buf.at[t], load_sem.at[t]
        )

    barrier = pltpu.get_barrier_semaphore()
    for t in range(1, n):
        pl.semaphore_signal(
            barrier, inc=1, device_id={"dom": lax.rem(me + t, n)},
            device_id_type=pl.DeviceIdType.MESH,
        )
    for t in range(1, groups):
        pl.semaphore_signal(
            barrier, inc=1, device_id={"shift": lax.rem(group + t, groups)},
            device_id_type=pl.DeviceIdType.MESH,
        )
    for t in range(n):
        load(t).start()
    pl.semaphore_wait(barrier, n - 1 + groups - 1)

    def halo(t, side):
        slot = lax.rem(group + groups - t, groups)
        if side == 0:
            planes, target, there = pl.ds(slab - HALO, HALO), pl.ds(0, HALO), right
        else:
            planes, target, there = pl.ds(0, HALO), pl.ds(slab + HALO, HALO), left
        if t == 0:
            src = src_ref.at[:, planes]
        else:
            start = slab if side == 0 else HALO
            src = wide_ref.at[slot, :, pl.ds(start, HALO)]
        return remote(
            src, wide_ref.at[slot, :, target], halo_send.at[t, side], halo_recv.at[t, side],
            dom=there,
        )

    def coeff_halo(which, side):
        ref = (kappa_ref, mass_ref)[which]
        if side == 0:
            planes, target, there = pl.ds(slab - HALO, HALO), pl.ds(0, HALO), right
        else:
            planes, target, there = pl.ds(0, HALO), pl.ds(slab + HALO, HALO), left
        return remote(
            ref.at[planes], coeff_ref.at[which, target], km_send.at[which, side],
            km_recv.at[which, side], dom=there,
        )

    def across(t):
        return remote(
            src_ref, wide_ref.at[group, :, pl.ds(HALO, slab)], z_send.at[t - 1], z_recv.at[t - 1],
            shift=lax.rem(group + t, groups),
        )

    @pl.when(has_right)
    def _():
        halo(0, 0).start()
        for which in range(2):
            coeff_halo(which, 0).start()

    @pl.when(has_left)
    def _():
        halo(0, 1).start()
        for which in range(2):
            coeff_halo(which, 1).start()

    for t in range(1, groups):
        across(t).start()

    wide_ref[group, :, pl.ds(HALO, slab)] = src_ref[...]
    coeff_ref[0, pl.ds(HALO, slab)] = kappa_ref[...]
    coeff_ref[1, pl.ds(HALO, slab)] = mass_ref[...]

    @pl.when(jnp.logical_not(has_left))
    def _():
        wide_ref[:, :, pl.ds(0, HALO)] = jnp.zeros(
            (groups, nb, HALO) + src_ref.shape[2:], jnp.float32
        )
        coeff_ref[:, pl.ds(0, HALO)] = jnp.zeros((2, HALO) + src_ref.shape[2:], jnp.float32)

    @pl.when(jnp.logical_not(has_right))
    def _():
        wide_ref[:, :, pl.ds(slab + HALO, HALO)] = jnp.zeros(
            (groups, nb, HALO) + src_ref.shape[2:], jnp.float32
        )
        coeff_ref[:, pl.ds(slab + HALO, HALO)] = jnp.zeros(
            (2, HALO) + src_ref.shape[2:], jnp.float32
        )

    @pl.when(has_left)
    def _():
        halo(0, 0).wait_recv()
        for which in range(2):
            coeff_halo(which, 0).wait_recv()

    @pl.when(has_right)
    def _():
        halo(0, 1).wait_recv()
        for which in range(2):
            coeff_halo(which, 1).wait_recv()

    low, high = edge_flags()
    mass = coeff_ref[1]
    diag = (6.0 - coeff_ref[0]) + MID * mass
    planes = slab + 2 * HALO
    grid_tail = src_ref.shape[2:]
    mask1 = plane_mask((planes - 2,) + grid_tail, 2, low, high)
    mask2 = plane_mask((planes - 4,) + grid_tail, 1, low, high)

    def one_source(b, carry):
        fields = basis_fields(wide_ref[group, b], diag, mass, mask1, mask2)
        for k, field in enumerate(fields):
            rounded = field.astype(jnp.bfloat16)
            raw_ref[k * nb + b] = rounded
            raw_ref[columns + k * nb + b] = (field - rounded.astype(jnp.float32)).astype(
                jnp.bfloat16
            )
        return carry

    lax.fori_loop(0, nb, one_source, 0)
    fields_ref[...] = raw_ref[...].reshape(fields_ref.shape)

    def forward(t):
        across(t).wait_recv()

        @pl.when(has_right)
        def _():
            halo(t, 0).start()

        @pl.when(has_left)
        def _():
            halo(t, 1).start()

    def scatter(t):
        return remote(
            out_buf.at[t], in_buf.at[t], rs_send.at[t], rs_recv.at[t],
            dom=lax.rem(me + 1 + t, n),
        )

    def multiply(t):
        load(t).wait()
        product = lax.dot_general(
            rows_buf[t].reshape(block, fields_ref.shape[1]), fields_ref[...],
            (((1,), (1,)), ((), ())), preferred_element_type=jnp.float32,
        )
        turned = product.T
        return turned[:columns] + turned[columns:]

    def step(t, carry):
        out_buf[t] = multiply(t)
        scatter(t).start()
        return carry

    lax.fori_loop(0, n - 1, step, 0)
    total = multiply(n - 1)
    for t in range(1, groups):
        forward(t)

    for t in range(n - 1):
        scatter(t).wait_recv()
        total = total + in_buf[t]

    lane = lax.broadcasted_iota(jnp.int32, (nb, LANES), 1)
    gram = jnp.zeros((nb, LANES), jnp.float32)
    for p, (i, k) in enumerate(PAIRS):
        value = jnp.sum(
            total[i * nb : (i + 1) * nb] * total[k * nb : (k + 1) * nb], axis=1, keepdims=True
        )
        gram = jnp.where(lane == p, value, gram)
    gram_own[...] = gram

    def share(t):
        return remote(
            gram_own, gram_in.at[t - 1], g_send.at[t - 1], g_recv.at[t - 1],
            dom=lax.rem(me + t, n),
        )

    for t in range(1, n):
        share(t).start()
    for t in range(1, n):
        share(t).wait_recv()
        gram = gram + gram_in[t - 1]
    gram_all[group] = gram

    def spread(t):
        return remote(
            gram_all.at[group], gram_all.at[group], s_send.at[t - 1], s_recv.at[t - 1],
            shift=lax.rem(group + t, groups),
        )

    for t in range(1, groups):
        spread(t).start()
    tau = jnp.zeros((1, LANES), jnp.float32)
    lane_row = lax.broadcasted_iota(jnp.int32, (1, LANES), 1)
    for j in range(ids_ref.shape[0]):
        tau = jnp.where(lane_row == j, table_ref[ids_ref[j]] - MID, tau)
    for t in range(1, groups):
        spread(t).wait_recv()
    count = groups * nb
    solved = coefficients(gram_all[...].reshape(count, LANES), tau)
    for i in range(3):
        c_ref[pl.ds(i * count, count)] = solved[i]

    for t in range(1, groups):
        @pl.when(has_left)
        def _():
            halo(t, 0).wait_recv()

        @pl.when(has_right)
        def _():
            halo(t, 1).wait_recv()

    @pl.when(has_right)
    def _():
        for t in range(groups):
            halo(t, 0).wait_send()
        for which in range(2):
            coeff_halo(which, 0).wait_send()

    @pl.when(has_left)
    def _():
        for t in range(groups):
            halo(t, 1).wait_send()
        for which in range(2):
            coeff_halo(which, 1).wait_send()

    for t in range(1, groups):
        across(t).wait_send()
        spread(t).wait_send()
    for t in range(n - 1):
        scatter(t).wait_send()
    for t in range(1, n):
        share(t).wait_send()


def combine_kernel(count, wide_ref, coeff_ref, c_ref, table_ref, ids_ref, sol_ref, res_ref):
    batch, planes = wide_ref.shape[0], wide_ref.shape[1]
    grid_tail = wide_ref.shape[2:]
    low, high = edge_flags()
    sixth = 1.0 / 6.0
    scaled1 = sixth * plane_mask((planes - 2,) + grid_tail, 2, low, high)
    scaled2 = sixth * plane_mask((planes - 4,) + grid_tail, 1, low, high)
    first = pl.program_id(0) * batch

    def one_source(i, carry):
        w0 = wide_ref[i]
        w0i = w0[1:-1]
        own = w0[3:-3]
        base = (6.0 - coeff_ref[0, 1:-1])
        near = neighbour_sum(w0)
        for j in range(ids_ref.shape[0]):
            sigma = table_ref[ids_ref[j]]
            center = 6.0 + sigma
            diag = base + sigma * coeff_ref[1, 1:-1]
            z0 = diag * w0i - near
            w1 = (z0 - center * w0i) * scaled1
            w1i = w1[1:-1]
            z1 = diag[1:-1] * w1i - neighbour_sum(w1)
            w2 = (z1 - center * w1i) * scaled2
            w2i = w2[1:-1]
            z2 = diag[2:-2] * w2i - neighbour_sum(w2)
            b = first + i
            c0 = c_ref[b, j]
            c1 = c_ref[count + b, j]
            c2 = c_ref[2 * count + b, j]
            sol_ref[j, i] = c0 * own + c1 * w1[2:-2] + c2 * w2i
            res_ref[j, i] = own - c0 * z0[2:-2] - c1 * z1[1:-1] - c2 * z2
        return carry

    lax.fori_loop(0, batch, one_source, 0)


def on_device(sources, kappa, mass, shift_table, shift_ids, sketch):
    n, groups = lax.axis_size("dom"), lax.axis_size("shift")
    nb, slab = sources.shape[0], sources.shape[1]
    tail = sources.shape[2:]
    shifts = shift_ids.shape[0]
    rows = sketch.shape[0]
    block = rows // n
    cells = slab * tail[0] * tail[1]
    planes = slab + 2 * HALO
    count = groups * nb
    columns = BASIS * nb
    vmem = pl.BlockSpec(memory_space=pltpu.VMEM)
    smem = pl.BlockSpec(memory_space=pltpu.SMEM)
    dma = pltpu.SemaphoreType.DMA
    f32 = jnp.float32
    wide, coeff, solved = pl.pallas_call(
        functools.partial(project_kernel, n, groups),
        out_shape=(
            jax.ShapeDtypeStruct((groups, nb, planes) + tail, f32),
            jax.ShapeDtypeStruct((2, planes) + tail, f32),
            jax.ShapeDtypeStruct((3 * count, LANES), f32),
        ),
        in_specs=[vmem, vmem, vmem, smem, smem, pl.BlockSpec(memory_space=pl.ANY)],
        out_specs=(vmem, vmem, vmem),
        scratch_shapes=[
            pltpu.VMEM((n, block, slab) + tail, jnp.bfloat16),
            pltpu.VMEM((2 * columns, slab) + tail, jnp.bfloat16),
            pltpu.VMEM((2 * columns, cells), jnp.bfloat16),
            pltpu.VMEM((n - 1, columns, block), f32),
            pltpu.VMEM((n - 1, columns, block), f32),
            pltpu.VMEM((nb, LANES), f32),
            pltpu.VMEM((n - 1, nb, LANES), f32),
            pltpu.VMEM((groups, nb, LANES), f32),
            dma((n,)),
            dma((groups - 1,)), dma((groups - 1,)),
            dma((groups, 2)), dma((groups, 2)),
            dma((2, 2)), dma((2, 2)),
            dma((n - 1,)), dma((n - 1,)),
            dma((n - 1,)), dma((n - 1,)),
            dma((groups - 1,)), dma((groups - 1,)),
        ],
        compiler_params=pltpu.CompilerParams(
            collective_id=0, has_side_effects=True, vmem_limit_bytes=56 << 20
        ),
        name="project",
    )(sources, kappa, mass, shift_table, shift_ids, sketch)

    batch = 4 if count % 4 == 0 else 1
    out = jax.ShapeDtypeStruct((shifts, count, slab) + tail, f32)
    out_spec = pl.BlockSpec((shifts, batch, slab) + tail, lambda i: (0, i, 0, 0, 0))
    return pl.pallas_call(
        functools.partial(combine_kernel, count),
        grid=(count // batch,),
        out_shape=(out, out),
        in_specs=[
            pl.BlockSpec((batch, planes) + tail, lambda i: (i, 0, 0, 0)),
            pl.BlockSpec((2, planes) + tail, lambda i: (0, 0, 0, 0)),
            smem, smem, smem,
        ],
        out_specs=(out_spec, out_spec),
        compiler_params=pltpu.CompilerParams(vmem_limit_bytes=32 << 20),
        name="combine",
    )(wide.reshape((count, planes) + tail), coeff, solved, shift_table, shift_ids)


def solution(mesh):
    placed = (
        P("shift", "dom", None, None),
        P("dom", None, None),
        P("dom", None, None),
        P(),
        P("shift"),
        P(None, "dom", None, None),
    )
    return jax.shard_map(
        on_device,
        mesh=mesh,
        in_specs=placed,
        out_specs=(P("shift", None, "dom", None, None), P("shift", None, "dom", None, None)),
        check_vma=False,
    )
```

profile of v0, /device:TPU:0, one launch (start us, length us, event | category | flops | bytes accessed | tf_op | source)
XLA Modules:
  0.0 66.3 jit_solution(5030699776044207980)
XLA Ops:
  0.6 0.0 copy-start.4
  0.6 0.0 copy-start.3
  0.7 46.4 %project.1 = (f32[4,8,10,16,128]{4,3,2,1,0:T(8,128)}, f32[2,10,16,128]{3,2,1,0:T(8,128)}, f32[96,128]{1,0:T(8,128)}) custom-call(f32[8,4,16,128]{3,2,1,0:T(8,128)} %src_ref.1, f32[4,16,128]{2,1,0:T(8,128)} %kappa_ref.1, f32[4,16,128]{2,1,0:T(8,128)} %mass_ref.1, f32[64]{0:T(128)} %table_ref.3, s32[4]{0:T(128)} %ids_ref.3, bf16[1024,4,16,128]{3,2,1,0:T(8,128)(2,1)} %sketch_ref.1), custom_call_target="tpu_custom_call" | custom-call | tf_op jit(solution)/shard_map/project/pallas_call | solution.py:421
  47.0 0.0 copy-done.4
  47.1 0.0 copy-done.3
  47.1 0.0 copy-start
  47.1 1.7 %copy-done = f32[4,8,10,16,128]{4,3,2,1,0:T(8,128)S(1)} copy-done((f32[4,8,10,16,128]{4,3,2,1,0:T(8,128)S(1)}, f32[4,8,10,16,128]{4,3,2,1,0:T(8,128)}, u32[]{:S(2)}) %copy-start) | copy-done | bytes 2621464
  48.8 0.0 copy-start.1
  48.8 0.9 %copy-done.1 = f32[2,10,16,128]{3,2,1,0:T(8,128)S(1)} copy-done((f32[2,10,16,128]{3,2,1,0:T(8,128)S(1)}, f32[2,10,16,128]{3,2,1,0:T(8,128)}, u32[]{:S(2)}) %copy-start.1) | copy-done | bytes 163864
  49.7 0.0 copy-start.2
  49.7 0.8 %copy-done.2 = f32[96,128]{1,0:T(8,128)S(1)} copy-done((f32[96,128]{1,0:T(8,128)S(1)}, f32[96,128]{1,0:T(8,128)}, u32[]{:S(2)}) %copy-start.2) | copy-done | bytes 49176
  50.5 15.8 %combine.1 = (f32[4,32,4,16,128]{4,3,2,1,0:T(8,128)}, f32[4,32,4,16,128]{4,3,2,1,0:T(8,128)}) custom-call(f32[32,10,16,128]{3,2,1,0:T(8,128)S(1)} %bitcast.1, f32[2,10,16,128]{3,2,1,0:T(8,128)S(1)} %copy-done.1, f32[96,128]{1,0:T(8,128)S(1)} %copy-done.2, f32[64]{0:T(128)S(1)} %copy-done.3, s32[4]{0:T(128)S(1)} %copy-done.4), custom_call_target="tpu_custom_call" | custom-call | tf_op jit(solution)/shard_map/combine/pallas_call | solution.py:456
Async XLA Ops:
  0.6 46.4 %copy-start.4 = (s32[4]{0:T(128)S(1)}, s32[4]{0:T(128)}, u32[]{:S(2)}) copy-start(s32[4]{0:T(128)} %ids_ref.3) | copy-start | bytes 52
  0.6 46.4 %copy-start.3 = (f32[64]{0:T(128)S(1)}, f32[64]{0:T(128)}, u32[]{:S(2)}) copy-start(f32[64]{0:T(128)} %table_ref.3) | copy-start | bytes 772
  47.1 1.7 %copy-start = (f32[4,8,10,16,128]{4,3,2,1,0:T(8,128)S(1)}, f32[4,8,10,16,128]{4,3,2,1,0:T(8,128)}, u32[]{:S(2)}) copy-start(f32[4,8,10,16,128]{4,3,2,1,0:T(8,128)} %get-tuple-element.5) | copy-start | bytes 7864324
  48.8 0.9 %copy-start.1 = (f32[2,10,16,128]{3,2,1,0:T(8,128)S(1)}, f32[2,10,16,128]{3,2,1,0:T(8,128)}, u32[]{:S(2)}) copy-start(f32[2,10,16,128]{3,2,1,0:T(8,128)} %get-tuple-element.6.coeff_ref) | copy-start | bytes 491524
  49.7 0.8 %copy-start.2 = (f32[96,128]{1,0:T(8,128)S(1)}, f32[96,128]{1,0:T(8,128)}, u32[]{:S(2)}) copy-start(f32[96,128]{1,0:T(8,128)} %get-tuple-element.7.c_ref) | copy-start | bytes 147460
where the time goes:
time: 66.6 us; the launch traced here: 66.3 us
  Pallas kernels  62.2 us (93%)
  local copies, waits for them, and re-layouts  3.45 us (5%)
  between operations  0.68 us (1%)
    pallas_call x1, Pallas kernels, on_device(): pl.pallas_call(functools.partial(project_kernel, n, groups), out_shape=(j...  46.4 us
    pallas_call x1, Pallas kernels, on_device(): pl.pallas_call(functools.partial(combine_kernel, count), grid=(count // b...  15.8 us
    unnamed x10, local copies, waits for them, and re-layouts  3.45 us

commit v1 on v0

--- a/solution.py
+++ b/solution.py
@@ -111,10 +111,10 @@
 
 
 def project_kernel(
-    n, groups, src_ref, kappa_ref, mass_ref, table_ref, ids_ref, sketch_ref,
+    n, groups, src_hbm, kappa_hbm, mass_hbm, table_ref, ids_ref, sketch_ref,
     wide_ref, coeff_ref, c_ref,
-    rows_buf, raw_ref, fields_ref, out_buf, in_buf, gram_own, gram_in, gram_all,
-    load_sem, z_send, z_recv, halo_send, halo_recv, km_send, km_recv,
+    src_ref, kappa_ref, mass_ref, mine_ref, rows_buf, raw_ref, fields_ref, out_buf, in_buf, gram_own, gram_in, gram_all,
+    load_sem, in_sem, own_sem, own_send, own_recv, z_send, z_recv, halo_send, halo_recv, km_send, km_recv,
     rs_send, rs_recv, g_send, g_recv, s_send, s_recv,
 ):
     me = lax.axis_index("dom")
@@ -148,73 +148,103 @@
             barrier, inc=1, device_id={"shift": lax.rem(group + t, groups)},
             device_id_type=pl.DeviceIdType.MESH,
         )
+    arguments = [
+        pltpu.make_async_copy(src_hbm, src_ref, in_sem.at[0]),
+        pltpu.make_async_copy(kappa_hbm, kappa_ref, in_sem.at[1]),
+        pltpu.make_async_copy(mass_hbm, mass_ref, in_sem.at[2]),
+    ]
+    for copy in arguments:
+        copy.start()
     for t in range(n):
         load(t).start()
+    for copy in arguments:
+        copy.wait()
     pl.semaphore_wait(barrier, n - 1 + groups - 1)
 
-    def halo(t, side):
-        slot = lax.rem(group + groups - t, groups)
+    def sides(side):
         if side == 0:
-            planes, target, there = pl.ds(slab - HALO, HALO), pl.ds(0, HALO), right
+            return slab - HALO, pl.ds(0, HALO), right
+        return 0, pl.ds(slab + HALO, HALO), left
+
+    def own_halo(side):
+        first, target, there = sides(side)
+        return remote(
+            src_ref.at[:, pl.ds(first, HALO)], mine_ref.at[:, target],
+            own_send.at[side], own_recv.at[side], dom=there,
+        )
+
+    hops = []
+    for k in range(1, groups // 2 + 1):
+        for way in range(2):
+            parts = (0, nb)
+            if 2 * k == groups:
+                parts = ((0, nb // 2), (nb // 2, nb - nb // 2))[way]
+            hops.append((way, k, pl.ds(*parts)))
+
+    def shifted(way, k):
+        step = k if way == 0 else groups - k
+        return lax.rem(group + step, groups)
+
+    def across(hop):
+        way, k, part = hop
+        if k == 1:
+            slot, src = group, src_ref.at[part]
         else:
-            planes, target, there = pl.ds(0, HALO), pl.ds(slab + HALO, HALO), left
-        if t == 0:
-            src = src_ref.at[:, planes]
-        else:
-            start = slab if side == 0 else HALO
-            src = wide_ref.at[slot, :, pl.ds(start, HALO)]
-        return remote(
-            src, wide_ref.at[slot, :, target], halo_send.at[t, side], halo_recv.at[t, side],
-            dom=there,
+            slot = shifted(1 - way, k - 1)
+            src = wide_ref.at[slot, part, pl.ds(HALO, slab)]
+        return remote(
+            src, wide_ref.at[slot, part, pl.ds(HALO, slab)],
+            z_send.at[way, k - 1], z_recv.at[way, k - 1], shift=shifted(way, 1),
+        )
+
+    def halo(hop, side):
+        way, k, part = hop
+        slot = shifted(1 - way, k)
+        first, target, there = sides(side)
+        return remote(
+            wide_ref.at[slot, part, pl.ds(HALO + first, HALO)], wide_ref.at[slot, part, target],
+            halo_send.at[way, k - 1, side], halo_recv.at[way, k - 1, side], dom=there,
         )
 
     def coeff_halo(which, side):
         ref = (kappa_ref, mass_ref)[which]
-        if side == 0:
-            planes, target, there = pl.ds(slab - HALO, HALO), pl.ds(0, HALO), right
-        else:
-            planes, target, there = pl.ds(0, HALO), pl.ds(slab + HALO, HALO), left
-        return remote(
-            ref.at[planes], coeff_ref.at[which, target], km_send.at[which, side],
+        first, target, there = sides(side)
+        return remote(
+            ref.at[pl.ds(first, HALO)], coeff_ref.at[which, target], km_send.at[which, side],
             km_recv.at[which, side], dom=there,
         )
 
-    def across(t):
-        return remote(
-            src_ref, wide_ref.at[group, :, pl.ds(HALO, slab)], z_send.at[t - 1], z_recv.at[t - 1],
-            shift=lax.rem(group + t, groups),
-        )
-
     @pl.when(has_right)
     def _():
-        halo(0, 0).start()
+        own_halo(0).start()
         for which in range(2):
             coeff_halo(which, 0).start()
 
     @pl.when(has_left)
     def _():
-        halo(0, 1).start()
+        own_halo(1).start()
         for which in range(2):
             coeff_halo(which, 1).start()
 
-    for t in range(1, groups):
-        across(t).start()
-
-    wide_ref[group, :, pl.ds(HALO, slab)] = src_ref[...]
+    for hop in hops:
+        if hop[1] == 1:
+            across(hop).start()
+
+    mine_ref[:, pl.ds(HALO, slab)] = src_ref[...]
     coeff_ref[0, pl.ds(HALO, slab)] = kappa_ref[...]
     coeff_ref[1, pl.ds(HALO, slab)] = mass_ref[...]
 
     @pl.when(jnp.logical_not(has_left))
     def _():
-        wide_ref[:, :, pl.ds(0, HALO)] = jnp.zeros(
-            (groups, nb, HALO) + src_ref.shape[2:], jnp.float32
+        mine_ref[:, pl.ds(0, HALO)] = jnp.zeros(
+            (nb, HALO) + src_ref.shape[2:], jnp.float32
         )
         coeff_ref[:, pl.ds(0, HALO)] = jnp.zeros((2, HALO) + src_ref.shape[2:], jnp.float32)
 
     @pl.when(jnp.logical_not(has_right))
     def _():
-        wide_ref[:, :, pl.ds(slab + HALO, HALO)] = jnp.zeros(
-            (groups, nb, HALO) + src_ref.shape[2:], jnp.float32
+        mine_ref[:, pl.ds(slab + HALO, HALO)] = jnp.zeros(
+            (nb, HALO) + src_ref.shape[2:], jnp.float32
         )
         coeff_ref[:, pl.ds(slab + HALO, HALO)] = jnp.zeros(
             (2, HALO) + src_ref.shape[2:], jnp.float32
@@ -222,16 +252,18 @@
 
     @pl.when(has_left)
     def _():
-        halo(0, 0).wait_recv()
+        own_halo(0).wait_recv()
         for which in range(2):
             coeff_halo(which, 0).wait_recv()
 
     @pl.when(has_right)
     def _():
-        halo(0, 1).wait_recv()
+        own_halo(1).wait_recv()
         for which in range(2):
             coeff_halo(which, 1).wait_recv()
 
+    keep = pltpu.make_async_copy(mine_ref, wide_ref.at[group], own_sem)
+    keep.start()
     low, high = edge_flags()
     mass = coeff_ref[1]
     diag = (6.0 - coeff_ref[0]) + MID * mass
@@ -241,7 +273,7 @@
     mask2 = plane_mask((planes - 4,) + grid_tail, 1, low, high)
 
     def one_source(b, carry):
-        fields = basis_fields(wide_ref[group, b], diag, mass, mask1, mask2)
+        fields = basis_fields(mine_ref[b], diag, mass, mask1, mask2)
         for k, field in enumerate(fields):
             rounded = field.astype(jnp.bfloat16)
             raw_ref[k * nb + b] = rounded
@@ -253,16 +285,24 @@
     lax.fori_loop(0, nb, one_source, 0)
     fields_ref[...] = raw_ref[...].reshape(fields_ref.shape)
 
-    def forward(t):
-        across(t).wait_recv()
+    def forward(hop):
+        across(hop).wait_recv()
+        for later in hops:
+            if later[0] == hop[0] and later[1] == hop[1] + 1:
+                across(later).start()
 
         @pl.when(has_right)
         def _():
-            halo(t, 0).start()
+            halo(hop, 0).start()
 
         @pl.when(has_left)
         def _():
-            halo(t, 1).start()
+            halo(hop, 1).start()
+
+    early = [hop for hop in hops if hop[1] < groups // 2]
+    late = [hop for hop in hops if hop[1] == groups // 2]
+    for hop in early:
+        forward(hop)
 
     def scatter(t):
         return remote(
@@ -286,8 +326,8 @@
 
     lax.fori_loop(0, n - 1, step, 0)
     total = multiply(n - 1)
-    for t in range(1, groups):
-        forward(t)
+    for hop in late:
+        forward(hop)
 
     for t in range(n - 1):
         scatter(t).wait_recv()
@@ -331,73 +371,93 @@
         spread(t).wait_recv()
     count = groups * nb
     solved = coefficients(gram_all[...].reshape(count, LANES), tau)
+    shifts = ids_ref.shape[0]
+    packed = jnp.zeros((count, LANES), jnp.float32)
+    lane_count = lax.broadcasted_iota(jnp.int32, (count, LANES), 1)
     for i in range(3):
-        c_ref[pl.ds(i * count, count)] = solved[i]
-
-    for t in range(1, groups):
+        value = jnp.where(lane_count < shifts, solved[i], 0.0)
+        packed = packed + (pltpu.roll(value, i * shifts, 1) if i else value)
+    c_ref[...] = packed
+
+    for hop in hops:
         @pl.when(has_left)
         def _():
-            halo(t, 0).wait_recv()
+            halo(hop, 0).wait_recv()
 
         @pl.when(has_right)
         def _():
-            halo(t, 1).wait_recv()
+            halo(hop, 1).wait_recv()
+
+    keep.wait()
 
     @pl.when(has_right)
     def _():
-        for t in range(groups):
-            halo(t, 0).wait_send()
+        own_halo(0).wait_send()
+        for hop in hops:
+            halo(hop, 0).wait_send()
         for which in range(2):
             coeff_halo(which, 0).wait_send()
 
     @pl.when(has_left)
     def _():
-        for t in range(groups):
-            halo(t, 1).wait_send()
+        own_halo(1).wait_send()
+        for hop in hops:
+            halo(hop, 1).wait_send()
         for which in range(2):
             coeff_halo(which, 1).wait_send()
 
     for t in range(1, groups):
-        across(t).wait_send()
         spread(t).wait_send()
+    for hop in hops:
+        across(hop).wait_send()
     for t in range(n - 1):
         scatter(t).wait_send()
     for t in range(1, n):
         share(t).wait_send()
 
 
-def combine_kernel(count, wide_ref, coeff_ref, c_ref, table_ref, ids_ref, sol_ref, res_ref):
+def combine_kernel(wide_ref, coeff_ref, c_ref, table_ref, ids_ref, sol_ref, res_ref, step_ref):
     batch, planes = wide_ref.shape[0], wide_ref.shape[1]
-    grid_tail = wide_ref.shape[2:]
-    low, high = edge_flags()
-    sixth = 1.0 / 6.0
-    scaled1 = sixth * plane_mask((planes - 2,) + grid_tail, 2, low, high)
-    scaled2 = sixth * plane_mask((planes - 4,) + grid_tail, 1, low, high)
+    me = lax.axis_index("dom")
+    has_low, has_high = me > 0, me < lax.axis_size("dom") - 1
+    shifts = ids_ref.shape[0]
     first = pl.program_id(0) * batch
 
+    def inside(field, width):
+        return jnp.concatenate(
+            [
+                jnp.where(has_low, field[:width], 0.0),
+                field[width:-width],
+                jnp.where(has_high, field[-width:], 0.0),
+            ],
+            axis=0,
+        )
+
+    @pl.when(pl.program_id(0) == 0)
+    def _():
+        for j in range(shifts):
+            sigma = table_ref[ids_ref[j]]
+            step_ref[j] = sigma * (coeff_ref[1, 1:-1] - 1.0) - coeff_ref[0, 1:-1]
+
     def one_source(i, carry):
-        w0 = wide_ref[i]
-        w0i = w0[1:-1]
+        w0 = inside(wide_ref[i], HALO)
         own = w0[3:-3]
-        base = (6.0 - coeff_ref[0, 1:-1])
         near = neighbour_sum(w0)
-        for j in range(ids_ref.shape[0]):
-            sigma = table_ref[ids_ref[j]]
-            center = 6.0 + sigma
-            diag = base + sigma * coeff_ref[1, 1:-1]
-            z0 = diag * w0i - near
-            w1 = (z0 - center * w0i) * scaled1
-            w1i = w1[1:-1]
-            z1 = diag[1:-1] * w1i - neighbour_sum(w1)
-            w2 = (z1 - center * w1i) * scaled2
-            w2i = w2[1:-1]
-            z2 = diag[2:-2] * w2i - neighbour_sum(w2)
-            b = first + i
+        b = first + i
+        for j in range(shifts):
+            center = 6.0 + table_ref[ids_ref[j]]
+            v1 = inside(step_ref[j] * w0[1:-1] - near, 2)
+            v2 = inside(step_ref[j, 1:-1] * v1[1:-1] - neighbour_sum(v1), 1)
+            v3 = step_ref[j, 2:-2] * v2[1:-1] - neighbour_sum(v2)
+            v1, v2 = v1[2:-2], v2[1:-1]
             c0 = c_ref[b, j]
-            c1 = c_ref[count + b, j]
-            c2 = c_ref[2 * count + b, j]
-            sol_ref[j, i] = c0 * own + c1 * w1[2:-2] + c2 * w2i
-            res_ref[j, i] = own - c0 * z0[2:-2] - c1 * z1[1:-1] - c2 * z2
+            c1 = c_ref[b, shifts + j] * (1.0 / 6.0)
+            c2 = c_ref[b, 2 * shifts + j] * (1.0 / 36.0)
+            sol_ref[j, i] = c0 * own + c1 * v1 + c2 * v2
+            res_ref[j, i] = (
+                (1.0 - c0 * center) * own - (c0 + c1 * center) * v1
+                - (c1 + c2 * center) * v2 - c2 * v3
+            )
         return carry
 
     lax.fori_loop(0, batch, one_source, 0)
@@ -415,6 +475,7 @@
     count = groups * nb
     columns = BASIS * nb
     vmem = pl.BlockSpec(memory_space=pltpu.VMEM)
+    hbm = pl.BlockSpec(memory_space=pl.ANY)
     smem = pl.BlockSpec(memory_space=pltpu.SMEM)
     dma = pltpu.SemaphoreType.DMA
     f32 = jnp.float32
@@ -423,11 +484,15 @@
         out_shape=(
             jax.ShapeDtypeStruct((groups, nb, planes) + tail, f32),
             jax.ShapeDtypeStruct((2, planes) + tail, f32),
-            jax.ShapeDtypeStruct((3 * count, LANES), f32),
+            jax.ShapeDtypeStruct((count, LANES), f32),
         ),
-        in_specs=[vmem, vmem, vmem, smem, smem, pl.BlockSpec(memory_space=pl.ANY)],
-        out_specs=(vmem, vmem, vmem),
+        in_specs=[hbm, hbm, hbm, smem, smem, hbm],
+        out_specs=(hbm, vmem, vmem),
         scratch_shapes=[
+            pltpu.VMEM(sources.shape, f32),
+            pltpu.VMEM(kappa.shape, f32),
+            pltpu.VMEM(mass.shape, f32),
+            pltpu.VMEM((nb, planes) + tail, f32),
             pltpu.VMEM((n, block, slab) + tail, jnp.bfloat16),
             pltpu.VMEM((2 * columns, slab) + tail, jnp.bfloat16),
             pltpu.VMEM((2 * columns, cells), jnp.bfloat16),
@@ -437,8 +502,10 @@
             pltpu.VMEM((n - 1, nb, LANES), f32),
             pltpu.VMEM((groups, nb, LANES), f32),
             dma((n,)),
-            dma((groups - 1,)), dma((groups - 1,)),
-            dma((groups, 2)), dma((groups, 2)),
+            dma((3,)), dma,
+            dma((2,)), dma((2,)),
+            dma((2, groups // 2)), dma((2, groups // 2)),
+            dma((2, groups // 2, 2)), dma((2, groups // 2, 2)),
             dma((2, 2)), dma((2, 2)),
             dma((n - 1,)), dma((n - 1,)),
             dma((n - 1,)), dma((n - 1,)),
@@ -454,7 +521,7 @@
     out = jax.ShapeDtypeStruct((shifts, count, slab) + tail, f32)
     out_spec = pl.BlockSpec((shifts, batch, slab) + tail, lambda i: (0, i, 0, 0, 0))
     return pl.pallas_call(
-        functools.partial(combine_kernel, count),
+        combine_kernel,
         grid=(count // batch,),
         out_shape=(out, out),
         in_specs=[
@@ -463,6 +530,7 @@
             smem, smem, smem,
         ],
         out_specs=(out_spec, out_spec),
+        scratch_shapes=[pltpu.VMEM((shifts, planes - 2) + tail, f32)],
         compiler_params=pltpu.CompilerParams(vmem_limit_bytes=32 << 20),
         name="combine",
     )(wide.reshape((count, planes) + tail), coeff, solved, shift_table, shift_ids)

time: 66.6 us -> 63.4 us (0.952)
  Pallas kernels: 62.2 us -> 59.1 us
    pallas_call x1, Pallas kernels: 46.4 us -> 44.5 us  [on_device(): pl.pallas_call(functools.partial(project_kernel, n, groups), out_shape=(j...]
    pallas_call x1, Pallas kernels: 15.8 us -> 14.6 us  [on_device(): pl.pallas_call(combine_kernel, grid=(count // batch,), out_shape=(out, ou...]
where the time goes in v1:
time: 63.4 us; the launch traced here: 63.2 us
  Pallas kernels  59.1 us (93%)
  local copies, waits for them, and re-layouts  3.37 us (5%)
  between operations  0.68 us (1%)
    pallas_call x1, Pallas kernels, on_device(): pl.pallas_call(functools.partial(project_kernel, n, groups), out_shape=(j...  44.5 us
    pallas_call x1, Pallas kernels, on_device(): pl.pallas_call(combine_kernel, grid=(count // batch,), out_shape=(out, ou...  14.6 us
    unnamed x10, local copies, waits for them, and re-layouts  3.37 us

profile of v1, /device:TPU:0, one launch (start us, length us, event | category | flops | bytes accessed | tf_op | source)
XLA Modules:
  0.0 63.2 jit_solution(15913392672803866578)
XLA Ops:
  0.6 0.0 copy-start.4
  0.6 0.0 copy-start.3
  0.7 44.5 %project.1 = (f32[4,8,10,16,128]{4,3,2,1,0:T(8,128)}, f32[2,10,16,128]{3,2,1,0:T(8,128)}, f32[32,128]{1,0:T(8,128)}) custom-call(f32[8,4,16,128]{3,2,1,0:T(8,128)} %src_hbm.1, f32[4,16,128]{2,1,0:T(8,128)} %kappa_hbm.1, f32[4,16,128]{2,1,0:T(8,128)} %mass_hbm.1, f32[64]{0:T(128)} %table_ref.3, s32[4]{0:T(128)} %ids_ref.3, bf16[1024,4,16,128]{3,2,1,0:T(8,128)(2,1)} %sketch_ref.1), custom_call_target="tpu_custom_call" | custom-call | tf_op jit(solution)/shard_map/project/pallas_call | solution.py:482
  45.2 0.0 copy-done.4
  45.2 0.0 copy-done.3
  45.2 0.0 copy-start
  45.2 1.7 %copy-done = f32[4,8,10,16,128]{4,3,2,1,0:T(8,128)S(1)} copy-done((f32[4,8,10,16,128]{4,3,2,1,0:T(8,128)S(1)}, f32[4,8,10,16,128]{4,3,2,1,0:T(8,128)}, u32[]{:S(2)}) %copy-start) | copy-done | bytes 2621464
  47.0 0.0 copy-start.1
  47.0 0.9 %copy-done.1 = f32[2,10,16,128]{3,2,1,0:T(8,128)S(1)} copy-done((f32[2,10,16,128]{3,2,1,0:T(8,128)S(1)}, f32[2,10,16,128]{3,2,1,0:T(8,128)}, u32[]{:S(2)}) %copy-start.1) | copy-done | bytes 163864
  47.9 0.0 copy-start.2
  47.9 0.7 %copy-done.2 = f32[32,128]{1,0:T(8,128)S(1)} copy-done((f32[32,128]{1,0:T(8,128)S(1)}, f32[32,128]{1,0:T(8,128)}, u32[]{:S(2)}) %copy-start.2) | copy-done | bytes 16408
  48.6 14.6 %combine.1 = (f32[4,32,4,16,128]{4,3,2,1,0:T(8,128)}, f32[4,32,4,16,128]{4,3,2,1,0:T(8,128)}) custom-call(f32[32,10,16,128]{3,2,1,0:T(8,128)S(1)} %bitcast.1, f32[2,10,16,128]{3,2,1,0:T(8,128)S(1)} %copy-done.1, f32[32,128]{1,0:T(8,128)S(1)} %copy-done.2, f32[64]{0:T(128)S(1)} %copy-done.3, s32[4]{0:T(128)S(1)} %copy-done.4), custom_call_target="tpu_custom_call" | custom-call | tf_op jit(solution)/shard_map/combine/pallas_call | solution.py:523
Async XLA Ops:
  0.6 44.6 %copy-start.4 = (s32[4]{0:T(128)S(1)}, s32[4]{0:T(128)}, u32[]{:S(2)}) copy-start(s32[4]{0:T(128)} %ids_ref.3) | copy-start | bytes 52
  0.6 44.6 %copy-start.3 = (f32[64]{0:T(128)S(1)}, f32[64]{0:T(128)}, u32[]{:S(2)}) copy-start(f32[64]{0:T(128)} %table_ref.3) | copy-start | bytes 772
  45.2 1.7 %copy-start = (f32[4,8,10,16,128]{4,3,2,1,0:T(8,128)S(1)}, f32[4,8,10,16,128]{4,3,2,1,0:T(8,128)}, u32[]{:S(2)}) copy-start(f32[4,8,10,16,128]{4,3,2,1,0:T(8,128)} %get-tuple-element.5) | copy-start | bytes 7864324
  47.0 0.9 %copy-start.1 = (f32[2,10,16,128]{3,2,1,0:T(8,128)S(1)}, f32[2,10,16,128]{3,2,1,0:T(8,128)}, u32[]{:S(2)}) copy-start(f32[2,10,16,128]{3,2,1,0:T(8,128)} %get-tuple-element.6.coeff_ref) | copy-start | bytes 491524
  47.9 0.7 %copy-start.2 = (f32[32,128]{1,0:T(8,128)S(1)}, f32[32,128]{1,0:T(8,128)}, u32[]{:S(2)}) copy-start(f32[32,128]{1,0:T(8,128)} %get-tuple-element.7.c_ref) | copy-start | bytes 49156

commit v2 on v1

--- a/solution.py
+++ b/solution.py
@@ -8,6 +8,7 @@
 from jax.sharding import PartitionSpec as P
 
 HALO = 3
+PIECES = 2
 LANES = 128
 MID = 2.25
 BASIS = 10
@@ -301,32 +302,40 @@
 
     early = [hop for hop in hops if hop[1] < groups // 2]
     late = [hop for hop in hops if hop[1] == groups // 2]
-    for hop in early:
-        forward(hop)
-
     def scatter(t):
         return remote(
             out_buf.at[t], in_buf.at[t], rs_send.at[t], rs_recv.at[t],
             dom=lax.rem(me + 1 + t, n),
         )
 
-    def multiply(t):
-        load(t).wait()
+    per = next(size for size in (PIECES, 2, 1) if n % size == 0)
+
+    def multiply(u):
+        for t in range(per):
+            load(u * per + t).wait()
         product = lax.dot_general(
-            rows_buf[t].reshape(block, fields_ref.shape[1]), fields_ref[...],
-            (((1,), (1,)), ((), ())), preferred_element_type=jnp.float32,
+            rows_buf[pl.ds(u * per, per)].reshape(per * block, fields_ref.shape[1]),
+            fields_ref[...], (((1,), (1,)), ((), ())), preferred_element_type=jnp.float32,
         )
         turned = product.T
-        return turned[:columns] + turned[columns:]
-
-    def step(t, carry):
-        out_buf[t] = multiply(t)
+        summed = turned[:columns] + turned[columns:]
+        return [summed[:, t * block : (t + 1) * block] for t in range(per)]
+
+    def send(t, piece):
+        out_buf[t] = piece
         scatter(t).start()
+
+    def step(u, carry):
+        for t, piece in enumerate(multiply(u)):
+            send(u * per + t, piece)
         return carry
 
-    lax.fori_loop(0, n - 1, step, 0)
-    total = multiply(n - 1)
-    for hop in late:
+    lax.fori_loop(0, n // per - 1, step, 0)
+    pieces = multiply(n // per - 1)
+    for t in range(per - 1):
+        send(n - per + t, pieces[t])
+    total = pieces[per - 1]
+    for hop in early:
         forward(hop)
 
     for t in range(n - 1):
@@ -354,6 +363,8 @@
         share(t).wait_recv()
         gram = gram + gram_in[t - 1]
     gram_all[group] = gram
+    for hop in late:
+        forward(hop)
 
     def spread(t):
         return remote(
@@ -531,7 +542,7 @@
         ],
         out_specs=(out_spec, out_spec),
         scratch_shapes=[pltpu.VMEM((shifts, planes - 2) + tail, f32)],
-        compiler_params=pltpu.CompilerParams(vmem_limit_bytes=32 << 20),
+        compiler_params=pltpu.CompilerParams(vmem_limit_bytes=63 << 20),
         name="combine",
     )(wide.reshape((count, planes) + tail), coeff, solved, shift_table, shift_ids)
 

time: 63.4 us -> 59.1 us (0.932)
  the two profiles are of different devices: /device:TPU:0 before, /device:TPU:1 now
where the time goes in v2:
time: 59.1 us; the launch traced here: 59 us
  Pallas kernels  58.3 us (99%)
  between operations  0.64 us (1%)
    pallas_call x1, Pallas kernels, on_device(): pl.pallas_call(functools.partial(project_kernel, n, groups), out_shape=(j...  43.4 us
    pallas_call x1, Pallas kernels, on_device(): pl.pallas_call(combine_kernel, grid=(count // batch,), out_shape=(out, ou...  14.9 us

profile of v2, /device:TPU:1, one launch (start us, length us, event | category | flops | bytes accessed | tf_op | source)
XLA Modules:
  0.0 59.0 jit_solution(1786756697881506854)
XLA Ops:
  0.6 43.4 %project.1 = (f32[4,8,10,16,128]{4,3,2,1,0:T(8,128)}, f32[2,10,16,128]{3,2,1,0:T(8,128)}, f32[32,128]{1,0:T(8,128)}) custom-call(f32[8,4,16,128]{3,2,1,0:T(8,128)} %src_hbm.1, f32[4,16,128]{2,1,0:T(8,128)} %kappa_hbm.1, f32[4,16,128]{2,1,0:T(8,128)} %mass_hbm.1, f32[64]{0:T(128)} %table_ref.3, s32[4]{0:T(128)} %ids_ref.3, bf16[1024,4,16,128]{3,2,1,0:T(8,128)(2,1)} %sketch_ref.1), custom_call_target="tpu_custom_call" | custom-call | tf_op jit(solution)/shard_map/project/pallas_call | solution.py:493
  44.0 14.9 %combine.1 = (f32[4,32,4,16,128]{4,3,2,1,0:T(8,128)}, f32[4,32,4,16,128]{4,3,2,1,0:T(8,128)}) custom-call(f32[32,10,16,128]{3,2,1,0:T(8,128)} %bitcast.1, f32[2,10,16,128]{3,2,1,0:T(8,128)} %get-tuple-element.6.coeff_ref, f32[32,128]{1,0:T(8,128)} %get-tuple-element.7.c_ref, f32[64]{0:T(128)} %table_ref.3, s32[4]{0:T(128)} %ids_ref.3), custom_call_target="tpu_custom_call" | custom-call | tf_op jit(solution)/shard_map/combine/pallas_call | solution.py:534
